TPU v7x, 32 devices: a whole 2x2x4 slice. The times are simulated.
32 devices in a mesh: tm: 4 (over y, x), space: 8 (over z, core).
Axes of the slice: x: 2, y: 2, z: 4, core: 2. Of those that a mesh axis runs over, the one named last changes fastest.
Arguments:
- queries: bfloat16 [4096, 4096], P(('tm', 'space')), may hold values from -20 to 20
- key_vectors: bfloat16 [4096, 4096], P(('tm', 'space')), may hold values from -20 to 20
- value_vectors: bfloat16 [4096, 4096], P(('tm', 'space')), may hold values from -6 to 6
- out_weight: bfloat16 [4096, 6144], P(None, 'space'), may hold values from -0.375 to 0.375
- frame_mask: int32 [4, 4], replicated, may hold values 0 or 1
Outputs:
- projected: bfloat16 [4096, 6144], P('tm', 'space')
All inputs are finite; a program needn't handle non-finite values.
Results may differ from a plain program's by a relative error of at most 0.0075.
Values may be sent and summed in bfloat16 or wider, within the bound.
A program may use at most 128 MiB of HBM per device.

v0:
```python
import math
import jax
import jax.numpy as jnp
from jax import lax
from jax.sharding import PartitionSpec as P

HD = 128


def passed_along(x, axis, by):
    devices = lax.axis_size(axis)
    return lax.ppermute(x, axis, [(i, (i + by) % devices) for i in range(devices)])


def block_update(state, query_blocks, arrived, allowed, scale_factor):
    run_max, run_total, run_sum = state
    keys_here = arrived[0]
    values_here = arrived[1]

    def one_block(pieces):
        query_part, old_max, old_total, old_sum = pieces
        scores = (
            jnp.einsum("qhd,khd->qhk", query_part, keys_here, preferred_element_type=jnp.float32)
            * scale_factor
        )
        block_max = jnp.where(allowed, jnp.max(scores, axis=2), -jnp.inf)
        new_max = jnp.maximum(old_max, block_max)
        exp_terms = jnp.where(allowed, jnp.exp(scores - new_max[:, :, None]), 0.0)
        rescale = jnp.exp(old_max - new_max)
        new_total = old_total * rescale + jnp.sum(exp_terms, axis=2)
        new_sum = old_sum * rescale[:, :, None] + jnp.einsum(
            "qhk,khd->qhd",
            exp_terms.astype(jnp.bfloat16),
            values_here,
            preferred_element_type=jnp.float32,
        )
        return (new_max, new_total, new_sum)

    return lax.map(one_block, (query_blocks, run_max, run_total, run_sum))


def mask_bit(frame_mask, row_index, column_index):
    count = frame_mask.shape[0]
    grid_rows = lax.broadcasted_iota(jnp.int32, (count, count), 0)
    grid_cols = lax.broadcasted_iota(jnp.int32, (count, count), 1)
    return jnp.sum(jnp.where((grid_rows == row_index) & (grid_cols == column_index), frame_mask, 0))


def body(queries, key_vectors, value_vectors, out_weight, frame_mask):
    frames = lax.axis_size("tm")
    here = lax.axis_index("tm")
    head_queries, head_keys, head_values = (
        lax.all_to_all(queries, "space", split_axis=1, concat_axis=0, tiled=True),
        lax.all_to_all(key_vectors, "space", split_axis=1, concat_axis=0, tiled=True),
        lax.all_to_all(value_vectors, "space", split_axis=1, concat_axis=0, tiled=True),
    )
    row_count = head_queries.shape[0]
    local_heads = head_queries.shape[1] // HD
    scale_factor = 1.0 / math.sqrt(HD)
    block_rows = 512
    block_count = row_count // block_rows
    query_blocks = head_queries.reshape(block_count, block_rows, local_heads, HD)
    pair = jnp.stack([head_keys, head_values]).reshape(2, row_count, local_heads, HD)
    state = (
        jnp.full((block_count, block_rows, local_heads), -jnp.inf, jnp.float32),
        jnp.zeros((block_count, block_rows, local_heads), jnp.float32),
        jnp.zeros((block_count, block_rows, local_heads, HD), jnp.float32),
    )
    state = block_update(state, query_blocks, pair, True, scale_factor)

    def visit(current, arrived, source):
        source_block = jnp.mod(source, frames)
        granted = mask_bit(frame_mask, here, source_block) == 1
        return block_update(current, query_blocks, arrived, granted, scale_factor)

    lower = pair
    upper = pair
    lower = passed_along(lower, "tm", 1)
    upper = passed_along(upper, "tm", -1)
    state = visit(state, lower, here - 1)
    state = visit(state, upper, here + 1)
    run_max, run_total, run_sum = state
    attended = (
        (run_sum / run_total[:, :, :, None])
        .reshape(row_count, local_heads * HD)
        .astype(jnp.bfloat16)
    )
    projected = jnp.dot(
        lax.all_gather(attended, "space", axis=1, tiled=True),
        out_weight,
        preferred_element_type=jnp.float32,
    )
    return projected.astype(jnp.bfloat16)


def solution(mesh):
    in_specs = (
        P(("tm", "space"), None),
        P(("tm", "space"), None),
        P(("tm", "space"), None),
        P(None, "space"),
        P(),
    )
    out_specs = P("tm", "space")
    return jax.shard_map(body, mesh=mesh, in_specs=in_specs, out_specs=out_specs, check_vma=False)
```

profile of v0, /device:TPU:0, one launch (start us, length us, event | category | flops | bytes accessed | tf_op | source)
XLA Modules:
  0.0 311.0 jit_solution(401340638023929092)
XLA Ops:
  6.5 2.3 copy.20
  8.9 6.4 %all-to-all-start.1 = ((bf16[128,8,512]{0,2,1:T(8,128)(2,1)}), bf16[128,8,512]{0,2,1:T(8,128)(2,1)S(1)}, u32[]{:S(2)}, u32[]{:S(2)}) async-start(bf16[128,8,512]{0,2,1:T(8,128)(2,1)} %bitcast.23), calls=%async_computation.1 | async-start | bytes 2097152 | tf_op jit(solution)/shard_map/all_to_all | solution.py:54
  15.2 2.3 copy.22
  17.5 24.3 %all-to-all-done.1 = bf16[128,8,512]{0,2,1:T(8,128)(2,1)S(1)} async-done(((bf16[128,8,512]{0,2,1:T(8,128)(2,1)}), bf16[128,8,512]{0,2,1:T(8,128)(2,1)S(1)}, u32[]{:S(2)}, u32[]{:S(2)}) %all-to-all-start.1) | async-done | bytes 1048608 | tf_op jit(solution)/shard_map/all_to_all | solution.py:54
  41.8 3.6 %all-to-all-start.2 = ((bf16[128,8,512]{0,2,1:T(8,128)(2,1)}), bf16[128,8,512]{0,2,1:T(8,128)(2,1)S(1)}, u32[]{:S(2)}, u32[]{:S(2)}) async-start(bf16[128,8,512]{0,2,1:T(8,128)(2,1)} %bitcast.25), calls=%async_computation.2 | async-start | bytes 2097152 | tf_op jit(solution)/shard_map/all_to_all | solution.py:55
  46.4 25.4 %all-to-all-done.2 = bf16[128,8,512]{0,2,1:T(8,128)(2,1)S(1)} async-done(((bf16[128,8,512]{0,2,1:T(8,128)(2,1)}), bf16[128,8,512]{0,2,1:T(8,128)(2,1)S(1)}, u32[]{:S(2)}, u32[]{:S(2)}) %all-to-all-start.2) | async-done | bytes 1048608 | tf_op jit(solution)/shard_map/all_to_all | solution.py:55
  72.8 3.6 %all-to-all-start = ((bf16[128,8,512]{2,0,1:T(8,128)(2,1)}), bf16[128,8,512]{2,0,1:T(8,128)(2,1)S(1)}, u32[]{:S(2)}, u32[]{:S(2)}) async-start(bf16[128,8,512]{2,0,1:T(8,128)(2,1)} %bitcast.193), calls=%async_computation | async-start | bytes 2097152 | tf_op jit(solution)/shard_map/all_to_all | solution.py:53
  81.8 2.0 copy.23
  86.3 2.3 constant_dynamic-update-slice_fusion.1
  88.6 2.3 constant_dynamic-update-slice_fusion
  93.8 9.1 %all-to-all-done = bf16[128,8,512]{2,0,1:T(8,128)(2,1)S(1)} async-done(((bf16[128,8,512]{2,0,1:T(8,128)(2,1)}), bf16[128,8,512]{2,0,1:T(8,128)(2,1)S(1)}, u32[]{:S(2)}, u32[]{:S(2)}) %all-to-all-start) | async-done | bytes 1048608 | tf_op jit(solution)/shard_map/all_to_all | solution.py:53
  107.1 11.4 %while.40 = (s32[]{:T(128)}, f32[2,512,4]{1,2,0:T(4,128)S(1)}, f32[2,512,4]{1,2,0:T(4,128)S(1)}, f32[2,512,4,128]{3,1,2,0:T(8,128)}, bf16[2,512,4,128]{3,1,2,0:T...) while((s32[]{:T(128)}, f32[2,512,4]{1,2,0:T(4,128)S(1)}, ...), condition=%wide.region_3.4_spmd, body=%wide.region_0.3_spmd.sunk | while | flops 1090787328 | bytes 45703320 | solution.py:39
  108.7 2.2 fusion.118
  110.9 1.9 fusion.116
  114.5 2.2 fusion.118
  118.6 22.0 %collective-permute-done = bf16[2,1024,4,128]{1,3,2,0:T(8,128)(2,1)} collective-permute-done((bf16[2,1024,4,128]{1,3,2,0:T(8,128)(2,1)}, bf16[2,1024,4,128]{1,3,2,0:T(8,128)(2,1)}, u32[]{:S(2)}, u32[]{:S(2)}) %collective-permute-start) | collective-permute-done | bytes 2097184 | tf_op jit(solution)/shard_map/ppermute | solution.py:12
  140.6 2.8 slice_bitcast_fusion.2
  147.8 13.7 %while.41 = (s32[]{:T(128)}, f32[2,512,4]{1,2,0:T(4,128)S(1)}, f32[2,512,4]{1,2,0:T(4,128)S(1)}, f32[2,512,4,128]{3,1,2,0:T(8,128)}, f32[2,512,4]{1,2,0:T(4,128)...) while((s32[]{:T(128)}, f32[2,512,4]{1,2,0:T(4,128)S(1)}, ...), condition=%wide.region_8.9_spmd, body=%wide.region_5.8_spmd.sunk | while | flops 1095249920 | bytes 59367672 | solution.py:39
  150.3 2.2 fusion.125
  152.5 2.1 fusion.123
  157.2 2.2 fusion.125
  159.4 2.1 fusion.123
  161.5 23.4 %collective-permute-done.1 = bf16[2,1024,4,128]{1,3,2,0:T(8,128)(2,1)} collective-permute-done((bf16[2,1024,4,128]{1,3,2,0:T(8,128)(2,1)}, bf16[2,1024,4,128]{1,3,2,0:T(8,128)(2,1)}, u32[]{:S(2)}, u32[]{:S(2)}) %collective-permute-start.1) | collective-permute-done | bytes 2097184 | tf_op jit(solution)/shard_map/ppermute | solution.py:12
  185.0 2.8 slice_bitcast_fusion
  192.2 13.7 %while.42 = (s32[]{:T(128)}, f32[2,512,4]{1,2,0:T(4,128)S(1)}, f32[2,512,4,128]{3,1,2,0:T(8,128)}, f32[2,512,4]{1,2,0:T(4,128)S(1)}, f32[2,512,4]{1,2,0:T(4,128)...) while((s32[]{:T(128)}, f32[2,512,4]{1,2,0:T(4,128)S(1)}, ...), condition=%wide.region_13.14_spmd, body=%wide.region_10.13_spmd.sunk | while | flops 1095249920 | bytes 59359472 | solution.py:39
  194.7 2.2 fusion.132
  196.9 2.1 fusion.130
  201.5 2.2 fusion.132
  203.8 2.1 fusion.130
  205.9 2.2 divide_convert_fusion
  210.1 82.4 %all-gather.2.cloned.1.call-done = bf16[1024,4096]{1,0:T(8,128)(2,1)} async-done(((bf16[1024,512]{1,0:T(8,128)(2,1)}), bf16[1024,4096]{1,0:T(8,128)(2,1)}) %all-gather.2.cloned.1.call-update) | async-done | bytes 8388624 | tf_op jit(solution)/shard_map/all_gather | solution.py:89
  292.4 11.8 %convolution_convert_fusion = bf16[1024,768]{1,0:T(8,128)(2,1)} fusion(bf16[1024,4096]{1,0:T(8,128)(2,1)} %all-gather.2.cloned.1.call-done, bf16[4096,768]{1,0:T(8,128)(2,1)} %param.14), kind=kOutput, calls=%fused_computation.78 | convolution fusion | flops 6443237376 | bytes 16252928 | tf_op jit(solution)/shard_map/dot_general | solution.py:88
  (98 shorter events, 41.6 us)
Async XLA Ops:
  6.5 38.8 %copy-start.10 = (bf16[128,4096]{1,0:T(8,128)(2,1)S(1)}, bf16[128,4096]{1,0:T(8,128)(2,1)}, u32[]{:S(2)}) copy-start(bf16[128,4096]{1,0:T(8,128)(2,1)} %param.11) | copy-start | bytes 3145732
  6.5 70.0 %copy-start.13 = (s32[4,4]{1,0:T(4,128)S(1)}, s32[4,4]{1,0:T(4,128)}, u32[]{:S(2)}) copy-start(s32[4,4]{1,0:T(4,128)} %param.15) | copy-start | bytes 196
  8.9 32.9 %all-to-all-start.1 = ((bf16[128,8,512]{0,2,1:T(8,128)(2,1)}), bf16[128,8,512]{0,2,1:T(8,128)(2,1)S(1)}, u32[]{:S(2)}, u32[]{:S(2)}) async-start(bf16[128,8,512]{0,2,1:T(8,128)(2,1)} %bitcast.23), calls=%async_computation.1 | async-start | bytes 2097152 | tf_op jit(solution)/shard_map/all_to_all | solution.py:54
  41.8 30.1 %all-to-all-start.2 = ((bf16[128,8,512]{0,2,1:T(8,128)(2,1)}), bf16[128,8,512]{0,2,1:T(8,128)(2,1)S(1)}, u32[]{:S(2)}, u32[]{:S(2)}) async-start(bf16[128,8,512]{0,2,1:T(8,128)(2,1)} %bitcast.25), calls=%async_computation.2 | async-start | bytes 2097152 | tf_op jit(solution)/shard_map/all_to_all | solution.py:55
  71.9 1.0 copy-start.2
  72.8 30.1 %all-to-all-start = ((bf16[128,8,512]{2,0,1:T(8,128)(2,1)}), bf16[128,8,512]{2,0,1:T(8,128)(2,1)S(1)}, u32[]{:S(2)}, u32[]{:S(2)}) async-start(bf16[128,8,512]{2,0,1:T(8,128)(2,1)} %bitcast.193), calls=%async_computation | async-start | bytes 2097152 | tf_op jit(solution)/shard_map/all_to_all | solution.py:53
  76.4 216.0 %all-gather.2.cloned.1.call-start = ((), (), s32[]{:S(2)}) async-start(), calls=%async_computation.3 | async-start | bytes 9437184 | tf_op jit(solution)/shard_map/all_gather | solution.py:89
  81.8 21.6 %copy-start.3 = (bf16[1024,4,128]{0,2,1:T(8,128)(2,1)S(1)}, bf16[1024,4,128]{0,2,1:T(8,128)(2,1)}, u32[]{:S(2)}) copy-start(bf16[1024,4,128]{0,2,1:T(8,128)(2,1)} %squeeze.55) | copy-start | bytes 3145732
  90.9 49.7 %collective-permute-start = (bf16[2,1024,4,128]{1,3,2,0:T(8,128)(2,1)}, bf16[2,1024,4,128]{1,3,2,0:T(8,128)(2,1)}, u32[]{:S(2)}, u32[]{:S(2)}) collective-permute-start(bf16[2,1024,4,128]{1,3,2,0:T(8,128)(2,1)} %constant_dynamic-update-slice_fusion), channel_id=1, source_target_pairs={{0,8},{8,16},{16,24},{24,0},{1,9},{9,17},{17,25},{25,1},{2,10},{10... | collective-permute-start | bytes 6291464 | tf_op jit(solution)/shard_map/ppermute | solution.py:12
  92.4 92.6 %collective-permute-start.1 = (bf16[2,1024,4,128]{1,3,2,0:T(8,128)(2,1)}, bf16[2,1024,4,128]{1,3,2,0:T(8,128)(2,1)}, u32[]{:S(2)}, u32[]{:S(2)}) collective-permute-start(bf16[2,1024,4,128]{1,3,2,0:T(8,128)(2,1)} %constant_dynamic-update-slice_fusion), channel_id=1, source_target_pairs={{0,24},{8,0},{16,8},{24,16},{1,25},{9,1},{17,9},{25,17},{2,26},{10... | collective-permute-start | bytes 6291464 | tf_op jit(solution)/shard_map/ppermute | solution.py:12
  107.1 1.6 copy-start.4
  110.9 1.9 copy-start.5
  112.9 1.6 copy-start.4
  116.7 1.9 copy-start.5
  147.8 1.6 copy-start.6
  147.8 2.2 copy-start.7
  147.8 2.5 copy-start.11
  152.5 2.1 copy-start.8
  154.7 1.6 copy-start.6
  154.7 2.2 copy-start.7
  154.7 2.5 copy-start.11
  159.4 2.1 copy-start.8
  192.2 1.6 copy-start
  192.2 2.2 copy-start.9
  192.2 2.5 copy-start.12
  196.9 2.1 copy-start.1
  199.0 1.6 copy-start
  199.0 2.2 copy-start.9
  199.1 2.5 copy-start.12
  203.8 2.1 copy-start.1
Sparse Core Ops, SparseCore 0:
  210.2 82.1 all-gather.1
where the time goes:
time: 312 us; the launch traced here: 311 us
  waiting for transfers between devices  187 us (60%)
  local copies, waits for them, and re-layouts  44.5 us (14%)
  matrix products  33.1 us (11%)
  starting transfers between devices  16.4 us (5%)
  other arithmetic  15.2 us (5%)
  between operations  14.9 us (5%)
    all_gather x1, waiting for transfers between devices, body(): lax.all_gather(attended, 'space', axis=1, tiled=True)  82.4 us
    ppermute x2, waiting for transfers between devices, passed_along(): lax.ppermute(x, axis, [(i, (i + by) % devices) for i in range(devices)])  45.5 us
    all_to_all x1, waiting for transfers between devices, body(): lax.all_to_all(value_vectors, 'space', split_axis=1, concat_axis=0, tiled...  25.4 us
    all_to_all x1, waiting for transfers between devices, body(): lax.all_to_all(key_vectors, 'space', split_axis=1, concat_axis=0, tiled=T...  24.3 us
    dot_general x6, matrix products, one_block(): jnp.einsum('qhk,khd->qhd', exp_terms.astype(jnp.bfloat16), values_here, p...  13.3 us
    reduce_sum x6, other arithmetic, one_block(): new_total = old_total * rescale + jnp.sum(exp_terms, axis=2)  12 us
    dot_general x1, matrix products, body(): jnp.dot(lax.all_gather(attended, 'space', axis=1, tiled=True), out_weight...  11.8 us
    all_to_all x1, waiting for transfers between devices, body(): lax.all_to_all(queries, 'space', split_axis=1, concat_axis=0, tiled=True)  9.06 us
  transfers between devices with their start and end apart: 6, of which 6 were waited for; matrix products, arithmetic and copies ran while one was open for 16% of the time, Pallas kernels for 0%

commit v1 on v0

--- a/solution.py
+++ b/solution.py
@@ -86,7 +86,7 @@
         .astype(jnp.bfloat16)
     )
     projected = jnp.dot(
-        lax.all_gather(attended, "space", axis=1, tiled=True),
+        jnp.concatenate(lax.all_gather(attended, "space"), axis=1),
         out_weight,
         preferred_element_type=jnp.float32,
     )

time: 312 us -> 324 us (1.038)
  local copies, waits for them, and re-layouts: 44.5 us -> 56 us
    all_gather x0 -> x1, local copies, waits for them, and re-layouts: none -> 11.4 us  [body(): lax.all_gather(attended, 'space')]
    unnamed x12 -> x11, local copies, waits for them, and re-layouts: 9.05 us -> 7.9 us
where the time goes in v1:
time: 324 us; the launch traced here: 323 us
  waiting for transfers between devices  187 us (58%)
  local copies, waits for them, and re-layouts  56 us (17%)
  matrix products  33.2 us (10%)
  starting transfers between devices  16.4 us (5%)
  other arithmetic  15.2 us (5%)
  between operations  14.9 us (5%)
    all_gather x1, waiting for transfers between devices, body(): lax.all_gather(attended, 'space')  82.4 us
    ppermute x2, waiting for transfers between devices, passed_along(): lax.ppermute(x, axis, [(i, (i + by) % devices) for i in range(devices)])  45.5 us
    all_to_all x1, waiting for transfers between devices, body(): lax.all_to_all(value_vectors, 'space', split_axis=1, concat_axis=0, tiled...  25.4 us
    all_to_all x1, waiting for transfers between devices, body(): lax.all_to_all(key_vectors, 'space', split_axis=1, concat_axis=0, tiled=T...  24.3 us
    dot_general x6, matrix products, one_block(): jnp.einsum('qhk,khd->qhd', exp_terms.astype(jnp.bfloat16), values_here, p...  13.3 us
    reduce_sum x6, other arithmetic, one_block(): new_total = old_total * rescale + jnp.sum(exp_terms, axis=2)  12 us
    dot_general x1, matrix products, body(): jnp.dot(jnp.concatenate(lax.all_gather(attended, 'space'), axis=1), out_w...  11.9 us
    all_gather x1, local copies, waits for them, and re-layouts, body(): lax.all_gather(attended, 'space')  11.4 us
  transfers between devices with their start and end apart: 6, of which 6 were waited for; matrix products, arithmetic and copies ran while one was open for 16% of the time, Pallas kernels for 0%

profile of v1, /device:TPU:0, one launch (start us, length us, event | category | flops | bytes accessed | tf_op | source)
XLA Modules:
  0.0 322.7 jit_solution(17438830157324887424)
XLA Ops:
  6.5 2.3 copy.21
  8.9 6.4 %all-to-all-start.1 = ((bf16[128,8,512]{0,2,1:T(8,128)(2,1)}), bf16[128,8,512]{0,2,1:T(8,128)(2,1)S(1)}, u32[]{:S(2)}, u32[]{:S(2)}) async-start(bf16[128,8,512]{0,2,1:T(8,128)(2,1)} %bitcast.23), calls=%async_computation.1 | async-start | bytes 2097152 | tf_op jit(solution)/shard_map/all_to_all | solution.py:54
  15.2 2.3 copy.23
  17.5 24.3 %all-to-all-done.1 = bf16[128,8,512]{0,2,1:T(8,128)(2,1)S(1)} async-done(((bf16[128,8,512]{0,2,1:T(8,128)(2,1)}), bf16[128,8,512]{0,2,1:T(8,128)(2,1)S(1)}, u32[]{:S(2)}, u32[]{:S(2)}) %all-to-all-start.1) | async-done | bytes 1048608 | tf_op jit(solution)/shard_map/all_to_all | solution.py:54
  41.8 3.6 %all-to-all-start.2 = ((bf16[128,8,512]{0,2,1:T(8,128)(2,1)}), bf16[128,8,512]{0,2,1:T(8,128)(2,1)S(1)}, u32[]{:S(2)}, u32[]{:S(2)}) async-start(bf16[128,8,512]{0,2,1:T(8,128)(2,1)} %bitcast.25), calls=%async_computation.2 | async-start | bytes 2097152 | tf_op jit(solution)/shard_map/all_to_all | solution.py:55
  46.4 25.4 %all-to-all-done.2 = bf16[128,8,512]{0,2,1:T(8,128)(2,1)S(1)} async-done(((bf16[128,8,512]{0,2,1:T(8,128)(2,1)}), bf16[128,8,512]{0,2,1:T(8,128)(2,1)S(1)}, u32[]{:S(2)}, u32[]{:S(2)}) %all-to-all-start.2) | async-done | bytes 1048608 | tf_op jit(solution)/shard_map/all_to_all | solution.py:55
  72.8 3.6 %all-to-all-start = ((bf16[128,8,512]{2,0,1:T(8,128)(2,1)}), bf16[128,8,512]{2,0,1:T(8,128)(2,1)S(1)}, u32[]{:S(2)}, u32[]{:S(2)}) async-start(bf16[128,8,512]{2,0,1:T(8,128)(2,1)} %bitcast.191), calls=%async_computation | async-start | bytes 2097152 | tf_op jit(solution)/shard_map/all_to_all | solution.py:53
  81.8 2.0 copy.24
  86.3 2.3 constant_dynamic-update-slice_fusion.1
  88.6 2.3 constant_dynamic-update-slice_fusion
  93.8 9.1 %all-to-all-done = bf16[128,8,512]{2,0,1:T(8,128)(2,1)S(1)} async-done(((bf16[128,8,512]{2,0,1:T(8,128)(2,1)}), bf16[128,8,512]{2,0,1:T(8,128)(2,1)S(1)}, u32[]{:S(2)}, u32[]{:S(2)}) %all-to-all-start) | async-done | bytes 1048608 | tf_op jit(solution)/shard_map/all_to_all | solution.py:53
  107.1 11.4 %while.40 = (s32[]{:T(128)}, f32[2,512,4]{1,2,0:T(4,128)S(1)}, f32[2,512,4]{1,2,0:T(4,128)S(1)}, f32[2,512,4,128]{3,1,2,0:T(8,128)}, bf16[2,512,4,128]{3,1,2,0:T...) while((s32[]{:T(128)}, f32[2,512,4]{1,2,0:T(4,128)S(1)}, ...), condition=%wide.region_3.4_spmd, body=%wide.region_0.3_spmd.sunk | while | flops 1090787328 | bytes 45703320 | solution.py:39
  108.7 2.2 fusion.118
  114.5 2.2 fusion.118
  118.6 22.0 %collective-permute-done = bf16[2,1024,4,128]{1,3,2,0:T(8,128)(2,1)} collective-permute-done((bf16[2,1024,4,128]{1,3,2,0:T(8,128)(2,1)}, bf16[2,1024,4,128]{1,3,2,0:T(8,128)(2,1)}, u32[]{:S(2)}, u32[]{:S(2)}) %collective-permute-start) | collective-permute-done | bytes 2097184 | tf_op jit(solution)/shard_map/ppermute | solution.py:12
  140.6 2.8 slice_bitcast_fusion.2
  147.8 13.7 %while.41 = (s32[]{:T(128)}, f32[2,512,4]{1,2,0:T(4,128)S(1)}, f32[2,512,4]{1,2,0:T(4,128)S(1)}, f32[2,512,4,128]{3,1,2,0:T(8,128)}, f32[2,512,4]{1,2,0:T(4,128)...) while((s32[]{:T(128)}, f32[2,512,4]{1,2,0:T(4,128)S(1)}, ...), condition=%wide.region_8.9_spmd, body=%wide.region_5.8_spmd.sunk | while | flops 1095249920 | bytes 59367672 | solution.py:39
  150.3 2.2 fusion.125
  152.5 2.1 fusion.123
  157.2 2.2 fusion.125
  159.4 2.1 fusion.123
  161.5 23.4 %collective-permute-done.1 = bf16[2,1024,4,128]{1,3,2,0:T(8,128)(2,1)} collective-permute-done((bf16[2,1024,4,128]{1,3,2,0:T(8,128)(2,1)}, bf16[2,1024,4,128]{1,3,2,0:T(8,128)(2,1)}, u32[]{:S(2)}, u32[]{:S(2)}) %collective-permute-start.1) | collective-permute-done | bytes 2097184 | tf_op jit(solution)/shard_map/ppermute | solution.py:12
  185.0 2.8 slice_bitcast_fusion
  192.2 13.7 %while.42 = (s32[]{:T(128)}, f32[2,512,4]{1,2,0:T(4,128)S(1)}, f32[2,512,4,128]{3,1,2,0:T(8,128)}, f32[2,512,4]{1,2,0:T(4,128)S(1)}, f32[2,512,4]{1,2,0:T(4,128)...) while((s32[]{:T(128)}, f32[2,512,4]{1,2,0:T(4,128)S(1)}, ...), condition=%wide.region_13.14_spmd, body=%wide.region_10.13_spmd.sunk | while | flops 1095249920 | bytes 59359472 | solution.py:39
  194.7 2.2 fusion.132
  196.9 2.1 fusion.130
  201.5 2.2 fusion.132
  203.8 2.1 fusion.130
  205.9 2.2 divide_convert_fusion
  210.1 82.4 %all-gather.2.cloned.1.call-done = bf16[8,1024,512]{2,1,0:T(8,128)(2,1)} async-done(((bf16[1,1024,512]{2,1,0:T(8,128)(2,1)}), bf16[8,1024,512]{2,1,0:T(8,128)(2,1)}) %all-gather.2.cloned.1.call-update) | async-done | bytes 8388624 | tf_op jit(solution)/shard_map/all_gather | solution.py:89
  292.5 11.4 %copy.37 = bf16[8,1024,512]{1,2,0:T(8,128)(2,1)} copy(bf16[8,1024,512]{2,1,0:T(8,128)(2,1)} %all-gather.2.cloned.1.call-done) | data formatting | bytes 16777216 | tf_op jit(solution)/shard_map/all_gather | solution.py:89
  303.9 11.9 %convolution_convert_fusion = bf16[1024,768]{1,0:T(8,128)(2,1)} fusion(bf16[1024,4096]{0,1:T(8,128)(2,1)} %bitcast.260, bf16[4096,768]{1,0:T(8,128)(2,1)} %param.14), kind=kOutput, calls=%fused_computation.78 | convolution fusion | flops 6443237376 | bytes 16252928 | tf_op jit(solution)/shard_map/dot_general | solution.py:88
  (99 shorter events, 43.6 us)
Async XLA Ops:
  6.5 38.8 %copy-start.10 = (bf16[128,4096]{1,0:T(8,128)(2,1)S(1)}, bf16[128,4096]{1,0:T(8,128)(2,1)}, u32[]{:S(2)}) copy-start(bf16[128,4096]{1,0:T(8,128)(2,1)} %param.11) | copy-start | bytes 3145732
  6.5 70.0 %copy-start.13 = (s32[4,4]{1,0:T(4,128)S(1)}, s32[4,4]{1,0:T(4,128)}, u32[]{:S(2)}) copy-start(s32[4,4]{1,0:T(4,128)} %param.15) | copy-start | bytes 196
  8.9 32.9 %all-to-all-start.1 = ((bf16[128,8,512]{0,2,1:T(8,128)(2,1)}), bf16[128,8,512]{0,2,1:T(8,128)(2,1)S(1)}, u32[]{:S(2)}, u32[]{:S(2)}) async-start(bf16[128,8,512]{0,2,1:T(8,128)(2,1)} %bitcast.23), calls=%async_computation.1 | async-start | bytes 2097152 | tf_op jit(solution)/shard_map/all_to_all | solution.py:54
  41.8 30.1 %all-to-all-start.2 = ((bf16[128,8,512]{0,2,1:T(8,128)(2,1)}), bf16[128,8,512]{0,2,1:T(8,128)(2,1)S(1)}, u32[]{:S(2)}, u32[]{:S(2)}) async-start(bf16[128,8,512]{0,2,1:T(8,128)(2,1)} %bitcast.25), calls=%async_computation.2 | async-start | bytes 2097152 | tf_op jit(solution)/shard_map/all_to_all | solution.py:55
  71.9 1.0 copy-start.2
  72.8 30.1 %all-to-all-start = ((bf16[128,8,512]{2,0,1:T(8,128)(2,1)}), bf16[128,8,512]{2,0,1:T(8,128)(2,1)S(1)}, u32[]{:S(2)}, u32[]{:S(2)}) async-start(bf16[128,8,512]{2,0,1:T(8,128)(2,1)} %bitcast.191), calls=%async_computation | async-start | bytes 2097152 | tf_op jit(solution)/shard_map/all_to_all | solution.py:53
  76.4 216.1 %all-gather.2.cloned.1.call-start = ((), (), s32[]{:S(2)}) async-start(), calls=%async_computation.3 | async-start | bytes 9437184 | tf_op jit(solution)/shard_map/all_gather | solution.py:89
  81.8 21.6 %copy-start.3 = (bf16[1024,4,128]{0,2,1:T(8,128)(2,1)S(1)}, bf16[1024,4,128]{0,2,1:T(8,128)(2,1)}, u32[]{:S(2)}) copy-start(bf16[1024,4,128]{0,2,1:T(8,128)(2,1)} %squeeze.55) | copy-start | bytes 3145732
  90.9 49.7 %collective-permute-start = (bf16[2,1024,4,128]{1,3,2,0:T(8,128)(2,1)}, bf16[2,1024,4,128]{1,3,2,0:T(8,128)(2,1)}, u32[]{:S(2)}, u32[]{:S(2)}) collective-permute-start(bf16[2,1024,4,128]{1,3,2,0:T(8,128)(2,1)} %constant_dynamic-update-slice_fusion), channel_id=1, source_target_pairs={{0,8},{8,16},{16,24},{24,0},{1,9},{9,17},{17,25},{25,1},{2,10},{10... | collective-permute-start | bytes 6291464 | tf_op jit(solution)/shard_map/ppermute | solution.py:12
  92.4 92.6 %collective-permute-start.1 = (bf16[2,1024,4,128]{1,3,2,0:T(8,128)(2,1)}, bf16[2,1024,4,128]{1,3,2,0:T(8,128)(2,1)}, u32[]{:S(2)}, u32[]{:S(2)}) collective-permute-start(bf16[2,1024,4,128]{1,3,2,0:T(8,128)(2,1)} %constant_dynamic-update-slice_fusion), channel_id=1, source_target_pairs={{0,24},{8,0},{16,8},{24,16},{1,25},{9,1},{17,9},{25,17},{2,26},{10... | collective-permute-start | bytes 6291464 | tf_op jit(solution)/shard_map/ppermute | solution.py:12
  107.1 1.6 copy-start.4
  110.9 1.9 copy-start.5
  112.9 1.6 copy-start.4
  116.7 1.9 copy-start.5
  147.8 1.6 copy-start.6
  147.8 2.2 copy-start.7
  147.8 2.5 copy-start.11
  152.5 2.1 copy-start.8
  154.7 1.6 copy-start.6
  154.7 2.2 copy-start.7
  154.7 2.5 copy-start.11
  159.4 2.1 copy-start.8
  192.2 1.6 copy-start
  192.2 2.2 copy-start.9
  192.2 2.5 copy-start.12
  196.9 2.1 copy-start.1
  199.0 1.6 copy-start
  199.0 2.2 copy-start.9
  199.1 2.5 copy-start.12
  203.8 2.1 copy-start.1
Sparse Core Ops, SparseCore 0:
  210.3 82.1 all-gather.1
